TPU v7x, 32 devices: a whole 2x2x4 slice. The times are simulated.
32 devices in a mesh: rows: 8 (over y, x, core), grp: 4 (over z).
Axes of the slice: x: 2, y: 2, z: 4, core: 2. Of those that a mesh axis runs over, the one named last changes fastest.
Arguments:
- momenta: float32 [128, 4, 24576], P('rows', 'grp'), may hold values from -6 to 6
Outputs:
- basis_out: float32 [128, 4, 24576], P(None, 'grp', 'rows')
- factor: float32 [128, 128], replicated
All inputs are finite; a program needn't handle non-finite values.
Results may differ from a plain program's by a relative error of at most 0.0003.
Values sent between devices are 32-bit elements; how exact they have to be, the bound alone decides.
No kernel may reach another device: no remote copies, remote signals or barrier semaphores. Data moves between devices by JAX's collectives and lax.ppermute only.
A program may use at most 192 MiB of HBM per device.

v0:
```python
import math
import jax
import jax.numpy as jnp
from jax import lax
from jax.sharding import PartitionSpec as P


def cross_products(left_mat, right_mat):
    return lax.dot_general(
        left_mat,
        right_mat,
        (((1,), (1,)), ((), ())),
        precision=lax.Precision.HIGHEST,
        preferred_element_type=jnp.float32,
    )


def upper_of(gram_matrix):
    return jnp.linalg.cholesky(gram_matrix).T


def lower_solve(lower_factor, right_hand):
    return lax.linalg.triangular_solve(lower_factor, right_hand, left_side=True, lower=True)


def on_device(momenta):
    voxel_panel = lax.all_to_all(momenta, "rows", split_axis=2, concat_axis=0, tiled=True)
    subject_rows = voxel_panel[:, 0, :]
    all_rows = subject_rows.shape[1] * lax.axis_size("rows") * lax.axis_size("grp")
    gram_matrix = cross_products(subject_rows, subject_rows)
    summed = lax.psum(gram_matrix, ("rows", "grp"))
    upper_factor = upper_of(summed)
    lower_factor = upper_factor.T
    ortho_t = lower_solve(lower_factor, subject_rows)
    scale = math.sqrt(all_rows)
    basis_out = (ortho_t * scale)[:, None, :]
    return (basis_out, upper_factor / scale)


def solution(mesh):
    return jax.shard_map(
        on_device,
        mesh=mesh,
        in_specs=(P("rows", "grp", None),),
        out_specs=(P(None, "grp", "rows"), P()),
        check_vma=False,
    )
```

profile of v0, /device:TPU:1, one launch (start us, length us, event | category | flops | bytes accessed | tf_op | source)
XLA Modules:
  0.0 378.4 jit_solution(2650943112555666837)
XLA Ops:
  7.2 0.0 all-reduce.2.cloned.1.call-start
  7.2 22.8 %copy.23 = f32[16,1,24576]{0,1,2:T(1,128)} copy(f32[16,1,24576]{2,1,0:T(1,128)} %param.1) | data formatting | bytes 3145728 | tf_op args[0]
  30.0 0.5 broadcast.50
  30.6 110.5 %reduce.6 = f32[24576,16]{1,0:T(8,128)} reduce(f32[24576,1,16]{2,1,0:T(1,128)} %bitcast.22, f32[]{:T(128)} %broadcast.50), dimensions={1}, to_apply=%bitcast.16.reduce_sub_computation | reduce | bytes 3145732
  141.1 8.9 %reshape.14 = f32[8,1,49152]{2,1,0:T(1,128)S(1)} reshape(f32[24576,16]{1,0:T(8,128)} %reduce.6) | data formatting | bytes 3145728
  149.9 24.7 %all_to_all.15 = f32[8,1,49152]{2,1,0:T(1,128)S(1)} all-to-all(f32[8,1,49152]{2,1,0:T(1,128)S(1)} %reshape.14), channel_id=1, replica_groups=mesh['rows'=8,'grp'=4] {'rows'}, dimensions={0} | all-to-all | bytes 3145728 | tf_op jit(solution)/shard_map/all_to_all | solution.py:27
  174.6 4.4 %reduce.7 = f32[8,49152]{1,0:T(8,128)S(1)} reduce(f32[8,1,49152]{2,1,0:T(1,128)S(1)} %all_to_all.15, f32[]{:T(128)} %broadcast.50), dimensions={1}, to_apply=%all_to_all.11.reduce_sub_computation | reduce | bytes 3145732 | tf_op jit(solution)/shard_map/all_to_all | solution.py:27
  179.0 30.7 %reshape.15 = f32[24576,1,16]{2,1,0:T(1,128)} reshape(f32[8,49152]{1,0:T(8,128)S(1)} %reduce.7) | data formatting | bytes 3145728
  209.8 7.6 %copy.31 = f32[16,1,8,3072]{3,2,0,1:T(8,128)S(1)} copy(f32[16,1,8,3072]{0,3,2,1:T(8,128)} %bitcast.21) | data formatting | bytes 3145728 | tf_op jit(solution)/shard_map/all_to_all | solution.py:27
  217.4 0.9 copy.25
  218.3 2.0 fusion.3
  220.4 0.0 all-reduce.2.cloned.1.call-update
  220.4 121.3 %all-reduce.2.cloned.1.call-done = f32[128,128]{0,1:T(8,128)} async-done(((f32[128,128]{0,1:T(8,128)}), f32[128,128]{0,1:T(8,128)}) %all-reduce.2.cloned.1.call-update) | async-done | bytes 65552 | tf_op jit(solution)/shard_map/psum | solution.py:31
  341.7 0.9 copy.27
  342.7 0.9 fusion.2
  343.5 11.7 %cholesky.16 = f32[128,128]{1,0:T(8,128)S(1)} custom-call(f32[128,128]{1,0:T(8,128)S(1)} %fusion.2), custom_call_target="Cholesky" | custom-call | tf_op jit(solution)/shard_map/jit(cholesky)/cholesky | solution.py:19
  355.3 0.6 compare_reduce_fusion
  355.9 0.7 multiply_bitcast_fusion
  356.6 0.7 copy.29
  357.3 9.8 %custom-call.6 = f32[1,128,128]{1,2,0:T(8,128)S(1)} custom-call(f32[1,128,128]{2,1,0:T(8,128)S(1)} %get-tuple-element.13), custom_call_target="InvertDiagBlocksLowerTriangular" | custom-call | tf_op jit(solution)/shard_map/triangular_solve | solution.py:23
  367.1 1.5 fusion
  368.6 2.8 copy.28
  (1 shorter events, 0.0 us)
Async XLA Ops:
  7.2 334.6 %all-reduce.2.cloned.1.call-start = ((), (), s32[]{:S(2)}) async-start(), calls=%async_computation.1 | async-start | bytes 131072 | tf_op jit(solution)/shard_map/psum | solution.py:31
Sparse Core Ops, SparseCore 0:
  220.5 121.1 all-reduce.1
where the time goes:
time: 385 us; the launch traced here: 378 us
  other arithmetic  139 us (36%)
  waiting for transfers between devices  121 us (31%)
  local copies, waits for them, and re-layouts  75.9 us (20%)
  blocking collectives  24.7 us (6%)
  between operations  14.3 us (4%)
    psum x1, waiting for transfers between devices, on_device(): summed = lax.psum(gram_matrix, ('rows', 'grp'))  121 us
    unnamed x1, other arithmetic  110 us
    unnamed x6, local copies, waits for them, and re-layouts  66.4 us
    all_to_all x1, blocking collectives, on_device(): lax.all_to_all(momenta, 'rows', split_axis=2, concat_axis=0, tiled=True)  24.7 us
    another operation x3, other arithmetic, upper_of(): return jnp.linalg.cholesky(gram_matrix).T  12.4 us
    another operation x1, other arithmetic, lower_solve(): lax.linalg.triangular_solve(lower_factor, right_hand, left_side=True, low...  9.81 us
    all_to_all x2, local copies, waits for them, and re-layouts, on_device(): lax.all_to_all(momenta, 'rows', split_axis=2, concat_axis=0, tiled=True)  8.56 us
  transfers between devices with their start and end apart: 1, of which 1 were waited for; matrix products, arithmetic and copies ran while one was open for 0% of the time, Pallas kernels for 0%

commit v1 on v0

--- a/solution.py
+++ b/solution.py
@@ -24,7 +24,10 @@
 
 
 def on_device(momenta):
-    voxel_panel = lax.all_to_all(momenta, "rows", split_axis=2, concat_axis=0, tiled=True)
+    voxel_panel = jnp.concatenate(
+        lax.all_to_all(jnp.stack(jnp.split(momenta, lax.axis_size("rows"), axis=2)), "rows", 0, 0),
+        axis=0,
+    )
     subject_rows = voxel_panel[:, 0, :]
     all_rows = subject_rows.shape[1] * lax.axis_size("rows") * lax.axis_size("grp")
     gram_matrix = cross_products(subject_rows, subject_rows)

time: 385 us -> 200 us (0.52); the launches traced: 378 us -> 200 us
  other arithmetic: 139 us -> 23.7 us
  local copies, waits for them, and re-layouts: 75.9 us -> 12.3 us
    unnamed x1 -> x0, other arithmetic: 110 us -> none
    unnamed x6 -> x10, local copies, waits for them, and re-layouts: 66.4 us -> 10.5 us
    all_to_all x2 -> x0, local copies, waits for them, and re-layouts: 8.56 us -> none  [on_device(): lax.all_to_all(momenta, 'rows', split_axis=2, concat_axis=0, tiled=True)]
    all_to_all x1 -> x0, other arithmetic: 4.38 us -> none  [on_device(): lax.all_to_all(momenta, 'rows', split_axis=2, concat_axis=0, tiled=True)]
where the time goes in v1:
time: 200 us
  waiting for transfers between devices  121 us (60%)
  blocking collectives  24.7 us (12%)
  other arithmetic  23.7 us (12%)
  between operations  14.1 us (7%)
  local copies, waits for them, and re-layouts  12.3 us (6%)
  matrix products  3.51 us (2%)
    psum x1, waiting for transfers between devices, on_device(): summed = lax.psum(gram_matrix, ('rows', 'grp'))  121 us
    all_to_all x1, blocking collectives, on_device(): lax.all_to_all(jnp.stack(jnp.split(momenta, lax.axis_size('rows'), axis=2...  24.7 us
    another operation x3, other arithmetic, upper_of(): return jnp.linalg.cholesky(gram_matrix).T  12.4 us
    unnamed x10, local copies, waits for them, and re-layouts  10.5 us
    another operation x1, other arithmetic, lower_solve(): lax.linalg.triangular_solve(lower_factor, right_hand, left_side=True, low...  9.81 us
  transfers between devices with their start and end apart: 1, of which 1 were waited for; matrix products, arithmetic and copies ran while one was open for 0% of the time, Pallas kernels for 0%

profile of v1, /device:TPU:1, one launch (start us, length us, event | category | flops | bytes accessed | tf_op | source)
XLA Modules:
  0.0 199.8 jit_solution(14320720991083701514)
XLA Ops:
  7.2 0.0 all-reduce.2.cloned.1.call-start
  7.2 0.9 bitcast_dynamic-update-slice_fusion.7
  8.2 1.0 bitcast_dynamic-update-slice_fusion.6
  9.1 1.0 bitcast_dynamic-update-slice_fusion.5
  10.1 1.0 bitcast_dynamic-update-slice_fusion.4
  11.0 1.0 bitcast_dynamic-update-slice_fusion.3
  12.0 1.0 bitcast_dynamic-update-slice_fusion.2
  13.0 1.0 bitcast_dynamic-update-slice_fusion.1
  13.9 1.0 bitcast_dynamic-update-slice_fusion
  14.9 24.7 %all_to_all.5 = f32[8,16,1,3072]{3,2,1,0:T(1,128)S(1)} all-to-all(f32[8,16,1,3072]{3,2,1,0:T(1,128)S(1)} %bitcast_dynamic-update-slice_fusion), channel_id=1, replica_groups=mesh['rows'=8,'grp'=4] {'rows'}, dimensions={0} | all-to-all | bytes 3145728 | tf_op jit(solution)/shard_map/all_to_all | solution.py:28
  39.6 0.3 copy.8
  39.9 2.0 %fusion.3 = f32[128,128]{0,1:T(8,128)} fusion(f32[128,3072]{1,0:T(8,128)S(1)} %bitcast.33), kind=kOutput, calls=%fused_computation.20 | convolution fusion | flops 603979776 | bytes 1638400 | tf_op jit(solution)/shard_map/dot_general | solution.py:9
  41.9 0.0 all-reduce.2.cloned.1.call-update
  41.9 121.3 %all-reduce.2.cloned.1.call-done = f32[128,128]{0,1:T(8,128)} async-done(((f32[128,128]{0,1:T(8,128)}), f32[128,128]{0,1:T(8,128)}) %all-reduce.2.cloned.1.call-update) | async-done | bytes 65552 | tf_op jit(solution)/shard_map/psum | solution.py:34
  163.3 0.9 copy.4
  164.2 0.9 fusion.2
  165.1 11.7 %cholesky.16 = f32[128,128]{1,0:T(8,128)S(1)} custom-call(f32[128,128]{1,0:T(8,128)S(1)} %fusion.2), custom_call_target="Cholesky" | custom-call | tf_op jit(solution)/shard_map/jit(cholesky)/cholesky | solution.py:19
  176.8 0.6 compare_reduce_fusion
  177.5 0.7 multiply_bitcast_fusion
  178.1 0.7 copy.6
  178.9 9.8 %custom-call.6 = f32[1,128,128]{1,2,0:T(8,128)S(1)} custom-call(f32[1,128,128]{2,1,0:T(8,128)S(1)} %get-tuple-element.5), custom_call_target="InvertDiagBlocksLowerTriangular" | custom-call | tf_op jit(solution)/shard_map/triangular_solve | solution.py:23
  188.7 1.5 fusion
  190.2 2.8 %copy.5 = f32[128,1,3072]{2,1,0:T(1,128)} copy(f32[128,1,3072]{2,0,1:T(8,128)S(1)} %fusion) | data formatting | bytes 3145728
  (1 shorter events, 0.0 us)
Async XLA Ops:
  7.2 156.1 %all-reduce.2.cloned.1.call-start = ((), (), s32[]{:S(2)}) async-start(), calls=%async_computation.1 | async-start | bytes 131072 | tf_op jit(solution)/shard_map/psum | solution.py:34
Sparse Core Ops, SparseCore 0:
  42.1 121.1 all-reduce.1
